TPU v7x, 256 devices: a whole 4x4x8 slice. The times are simulated.
256 devices in a mesh: group: 64 (over z, y_hi, x), replica: 4 (over y_lo, core).
Axes of the slice: x: 4, y: 4 (y_hi: 2, y_lo: 2; y = y_hi * 2 + y_lo), z: 8, core: 2. Of those that a mesh axis runs over, the one named last changes fastest.
Arguments:
- grad: bfloat16 [32768, 8192], P('group', 'replica'), may hold values from -45 to 45, as said below
- prev_left: bfloat16 [64, 512, 512], P('group', 'replica'), may hold values from -1 to 1.5
- prev_right: bfloat16 [16, 512, 512], P('replica', 'group'), may hold values from -1 to 1.5
- exp_left: int32 [64], P('group'), may hold values from -2 to 2
- exp_right: int32 [16], P('replica'), may hold values from -2 to 2
- strip_owner: int32 [64], replicated, may hold values from 0 to 63, each once
Outputs:
- precond: bfloat16 [32768, 8192], P('group', 'replica')
- root_left: bfloat16 [64, 512, 512], P('group', 'replica')
- root_right: bfloat16 [16, 64, 8, 512], P('replica', 'group')
Inputs may be any that keep to these rules, and one draw needn't show every extreme that they name: `grad`: entries have row and column scales of different sizes. `strip_owner`: each of 0 to 63 appears once.
All inputs are finite; a program needn't handle non-finite values.
Results may differ from a plain program's by a relative error of at most 0.0083.
Values may be sent and summed in bfloat16 or wider, within the bound.
A program may use at most 64 MiB of HBM per device.

v0:
```python
import jax
import jax.numpy as jnp
from jax import lax
from jax.sharding import Mesh
from jax.sharding import PartitionSpec as P

GROUP = ("group_0", "group_1", "group_2")
REPLICA = ("replica_0", "replica_1")
GROUP_REPLICA = ("group_0", "group_1", "group_2", "replica_0", "replica_1")


EPSILON = 1e-06


def over_axes(x, axes):
    for axis in axes:
        x = lax.psum(x, axis)
    return x


def cut_along(x, dim, devices):
    dims = x.shape
    pieces = x.reshape(*dims[:dim], devices, dims[dim] // devices, *dims[dim + 1 :])
    return jnp.moveaxis(pieces, dim, 0)


def sent_and_summed(x, axis, dim):
    pieces = cut_along(x, dim, lax.axis_size(axis))
    arrived = lax.all_to_all(pieces, axis, split_axis=0, concat_axis=0, tiled=True)
    return arrived.astype(jnp.float32).sum(axis=0)


def from_everyone(x, axis):
    copies = jnp.broadcast_to(x, (lax.axis_size(axis), *x.shape))
    return lax.all_to_all(copies, axis, split_axis=0, concat_axis=0, tiled=True)


def in_order(pieces, dim):
    pieces = jnp.moveaxis(pieces, 0, dim)
    dims = pieces.shape
    return pieces.reshape(*dims[:dim], dims[dim] * dims[dim + 1], *dims[dim + 2 :])


def collect(x, axis, dim):
    pieces = from_everyone(x, axis)
    return in_order(pieces, dim)


def pow_two(exponent):
    result = jnp.zeros(exponent.shape, jnp.float32)
    for power in range(-4, 5):
        result = result + jnp.where(exponent == power, jnp.float32(2.0**power), jnp.float32(0.0))
    return result


def newton_rows(gram_rows, gram_scale, start_root, start_rows):
    product = gram_rows / gram_scale
    for repeat in range(5):
        product = jnp.matmul(product, start_root, precision=lax.Precision.HIGHEST)
    return (5.0 * start_rows - product) / 4.0


def shards(grad, prev_left, prev_right, exp_left, exp_right, strip_owner):
    block_size = grad.shape[0]
    col_count = prev_right.shape[0]
    pieces = grad.reshape(block_size, col_count, block_size)
    groups = lax.axis_size(GROUP)
    replicas = lax.axis_size(REPLICA)
    group_index = lax.axis_index(GROUP)
    replica_index = lax.axis_index(REPLICA)
    strip_rows = block_size // groups
    square = jnp.sum(jnp.square(pieces.astype(jnp.float32)), axis=(0, 2))
    group_pick = (jnp.arange(groups) == group_index).astype(jnp.float32)
    replica_pick = (jnp.arange(replicas) == replica_index).astype(jnp.float32)
    norm_grid = group_pick[:, None, None] * replica_pick[None, :, None] * square[None, None, :]
    norm_grid = over_axes(norm_grid, GROUP_REPLICA)
    left_scale = jnp.sum(norm_grid * group_pick[:, None, None]) / block_size + EPSILON
    right_scale = (
        jnp.sum(norm_grid * replica_pick[None, :, None], axis=(0, 1)) / block_size + EPSILON
    )
    left_part = lax.dot_general(
        grad, grad, (((1,), (1,)), ((), ())), preferred_element_type=jnp.float32
    )
    right_part = lax.dot_general(
        pieces, pieces, (((0,), (0,)), ((1,), (1,))), preferred_element_type=jnp.float32
    )
    left_strip = sent_and_summed(left_part.astype(jnp.bfloat16), REPLICA, 0)
    owned_strip = strip_owner[group_index]
    reordered = right_part.reshape(col_count, groups, strip_rows, block_size)[:, strip_owner]
    reordered = reordered.reshape(col_count, block_size, block_size)
    right_strip = sent_and_summed(reordered.astype(jnp.bfloat16), GROUP, 1)
    left_start = collect(prev_left[0], REPLICA, 0).astype(jnp.float32)
    right_start = lax.all_gather(prev_right, GROUP, axis=1, tiled=True).astype(jnp.float32)
    left_rows = prev_left[0].astype(jnp.float32)
    right_rows = lax.dynamic_slice_in_dim(right_start, owned_strip * strip_rows, strip_rows, 1)
    left_new = newton_rows(left_strip, left_scale, left_start, left_rows)
    right_new = newton_rows(right_strip, right_scale[:, None, None], right_start, right_rows)
    left_code = (left_new * pow_two(-exp_left[0])).astype(jnp.bfloat16)
    right_code = (right_new * pow_two(-exp_right)[:, None, None]).astype(jnp.bfloat16)
    left_full = collect(left_code, REPLICA, 0)
    right_owned = lax.all_gather(right_code, GROUP, axis=1, tiled=True).reshape(
        col_count, groups, strip_rows, block_size
    )
    owner_match = strip_owner[:, None] == jnp.arange(groups)[None, :]
    inverse = jnp.sum(jnp.where(owner_match, jnp.arange(groups)[:, None], 0), axis=0)
    right_full = right_owned[:, inverse].reshape(col_count, block_size, block_size)
    left_dec = (left_full.astype(jnp.float32) * pow_two(exp_left[0])).astype(jnp.bfloat16)
    right_dec = (right_full.astype(jnp.float32) * pow_two(exp_right)[:, None, None]).astype(
        jnp.bfloat16
    )
    middle = lax.dot_general(
        pieces, right_dec, (((2,), (1,)), ((1,), (0,))), preferred_element_type=jnp.float32
    ).astype(jnp.bfloat16)
    result = lax.dot_general(
        left_dec, middle, (((1,), (1,)), ((), ())), preferred_element_type=jnp.float32
    ).astype(jnp.bfloat16)
    return (
        result.reshape(block_size, col_count * block_size),
        left_code[None],
        right_code[:, None],
    )


def solution(mesh):
    torus = Mesh(
        mesh.devices.reshape(8, 2, 4, 2, 2),
        ("group_0", "group_1", "group_2", "replica_0", "replica_1"),
    )
    in_specs = (
        P(GROUP, REPLICA),
        P(GROUP, REPLICA, None),
        P(REPLICA, GROUP, None),
        P(GROUP),
        P(REPLICA),
        P(),
    )
    out_specs = (P(GROUP, REPLICA), P(GROUP, REPLICA, None), P(REPLICA, GROUP, None, None))
    return jax.shard_map(
        shards, mesh=torus, in_specs=in_specs, out_specs=out_specs, check_vma=False
    )
```

profile of v0, /device:TPU:32, one launch (start us, length us, event | category | flops | bytes accessed | tf_op | source)
XLA Modules:
  0.0 277.9 jit_solution(7575325970475510265)
XLA Ops:
  7.2 0.0 copy-start.5
  7.2 3.5 %convolution_bitcast_fusion = bf16[4,64,8,512]{3,2,1,0:T(8,128)(2,1)S(1)} fusion(bf16[64,4,8,512]{3,2,1,0:T(8,128)(2,1)} %bitcast.77), kind=kOutput, calls=%fused_computation.7 | convolution fusion | flops 1073741824 | bytes 4194304 | tf_op jit(solution)/shard_map/dot_general | solution.py:84
  10.7 0.0 copy-done.5
  10.8 2.0 gather_fusion
  12.8 14.2 %all-to-all-start.3 = ((bf16[64,4,8,512]{3,2,1,0:T(8,128)(2,1)}), bf16[64,4,8,512]{3,2,1,0:T(8,128)(2,1)S(1)}, u32[]{:S(2)}, u32[]{:S(2)}) async-start(bf16[64,4,8,512]{3,2,1,0:T(8,128)(2,1)} %gather_fusion), calls=%async_computation.3 | async-start | bytes 4194304 | tf_op jit(solution)/shard_map/all_to_all | solution.py:29
  27.0 0.0 copy-start.4
  27.0 0.0 all-gather.3.cloned.1.call-start
  27.1 0.7 all-gather.3.cloned.1.call-update
  27.7 0.0 all-gather.5.cloned.1.call-start
  27.8 0.6 dynamic_slice.6
  29.0 2.0 multiply_reduce_fusion
  31.1 0.1 reduce_sum.66
  31.2 0.1 broadcast_multiply_fusion.1
  31.3 0.1 broadcast_multiply_fusion
  31.4 51.7 %psum.35 = f32[64,4,4]{0,2,1:T(4,128)S(1)} all-reduce(f32[64,4,4]{0,2,1:T(4,128)S(1)} %broadcast_multiply_fusion), channel_id=1, replica_groups=mesh['group_0'=8,'group_1'=2,'group_2'=4,'replica_0'=2,'replica_1'=2] {'..., use_global_device_ids=true, to_apply=%region_3.0 | all-reduce | flops 1024 | bytes 8192 | tf_op jit(solution)/shard_map/psum | solution.py:17
  83.1 6.5 %psum.36 = f32[64,4,4]{0,2,1:T(4,128)S(1)} all-reduce(f32[64,4,4]{0,2,1:T(4,128)S(1)} %psum.35), channel_id=1, replica_groups=mesh['group_0'=8,'group_1'=2,'group_2'=4,'replica_0'=2,'replica_1'=2] {'..., use_global_device_ids=true, to_apply=%region_4.0 | all-reduce | flops 1024 | bytes 8192 | tf_op jit(solution)/shard_map/psum | solution.py:17
  89.6 10.5 %psum.37 = f32[64,4,4]{0,2,1:T(4,128)S(1)} all-reduce(f32[64,4,4]{0,2,1:T(4,128)S(1)} %psum.36), channel_id=1, replica_groups=mesh['group_0'=8,'group_1'=2,'group_2'=4,'replica_0'=2,'replica_1'=2] {'..., use_global_device_ids=true, to_apply=%region_5.0 | all-reduce | flops 1024 | bytes 8192 | tf_op jit(solution)/shard_map/psum | solution.py:17
  100.2 5.0 %psum.38 = f32[64,4,4]{0,2,1:T(4,128)S(1)} all-reduce(f32[64,4,4]{0,2,1:T(4,128)S(1)} %psum.37), channel_id=1, replica_groups=mesh['group_0'=8,'group_1'=2,'group_2'=4,'replica_0'=2,'replica_1'=2] {'..., use_global_device_ids=true, to_apply=%region_6.0 | all-reduce | flops 1024 | bytes 8192 | tf_op jit(solution)/shard_map/psum | solution.py:17
  105.2 2.5 psum.39
  107.6 0.6 multiply_reduce_fusion.1
  108.2 0.0 copy-done.4
  108.3 0.0 all-to-all-done.3
  108.3 0.3 convert_reduce_fusion
  108.6 36.5 %all-gather.3.cloned.1.call-done = bf16[4,512,512]{2,1,0:T(8,128)(2,1)} async-done(((bf16[4,8,512]{2,1,0:T(8,128)(2,1)}), bf16[4,512,512]{2,1,0:T(8,128)(2,1)}) %all-gather.3.cloned.1.call-update) | async-done | bytes 2097168 | tf_op jit(solution)/shard_map/all_gather | solution.py:93
  145.1 0.0 copy-start
  145.1 2.7 fusion.29
  147.8 0.0 copy-done
  147.8 0.9 fusion.53
  148.8 0.9 fusion.54
  149.7 0.0 copy-start.1
  149.7 0.9 fusion.55
  150.6 1.6 fusion.25
  152.2 0.0 all-gather.5.cloned.1.call-update
  152.2 0.0 copy-done.1
  152.2 0.0 copy-start.2
  152.2 1.3 convolution_convert_fusion
  153.5 11.3 %all_to_all.20 = bf16[4,128,512]{2,1,0:T(8,128)(2,1)S(1)} all-to-all(bf16[4,128,512]{2,1,0:T(8,128)(2,1)S(1)} %bitcast.81), channel_id=1, replica_groups=mesh['group_0'=8,'group_1'=2,'group_2'=4,'replica_0'=2,'replica_1'=2] {'..., dimensions={0} | all-to-all | bytes 1048576 | tf_op jit(solution)/shard_map/all_to_all | solution.py:29
  164.8 0.0 copy-done.2
  164.8 0.8 broadcast_in_dim.97
  165.6 3.5 %all-to-all-start.1 = ((bf16[4,128,512]{2,1,0:T(8,128)(2,1)}), bf16[4,128,512]{2,1,0:T(8,128)(2,1)S(1)}, u32[]{:S(2)}, u32[]{:S(2)}) async-start(bf16[4,128,512]{2,1,0:T(8,128)(2,1)} %broadcast_in_dim.97), calls=%async_computation.1 | async-start | bytes 1048576 | tf_op jit(solution)/shard_map/all_to_all | solution.py:35
  170.5 0.1 convert_reduce_fusion.1
  170.5 7.3 %all-to-all-done.1 = bf16[4,128,512]{2,1,0:T(8,128)(2,1)S(1)} async-done(((bf16[4,128,512]{2,1,0:T(8,128)(2,1)}), bf16[4,128,512]{2,1,0:T(8,128)(2,1)S(1)}, u32[]{:S(2)}, u32[]{:S(2)}) %all-to-all-start.1) | async-done | bytes 524320 | tf_op jit(solution)/shard_map/all_to_all | solution.py:35
  177.9 0.4 fusion.26
  178.2 0.4 fusion.50
  178.6 0.4 fusion.51
  179.0 0.4 fusion.52
  179.4 0.4 fusion.23
  179.8 0.0 copy-start.3
  179.8 0.8 broadcast_in_dim.98
  180.6 3.7 %all-to-all-start.2 = ((bf16[4,128,512]{2,1,0:T(8,128)(2,1)}), bf16[4,128,512]{2,1,0:T(8,128)(2,1)S(1)}, u32[]{:S(2)}, u32[]{:S(2)}) async-start(bf16[4,128,512]{2,1,0:T(8,128)(2,1)} %broadcast_in_dim.98), calls=%async_computation.2 | async-start | bytes 1048576 | tf_op jit(solution)/shard_map/all_to_all | solution.py:35
  184.3 0.1 select_reduce_fusion
  184.4 8.5 %all-to-all-done.2 = bf16[4,128,512]{2,1,0:T(8,128)(2,1)S(1)} async-done(((bf16[4,128,512]{2,1,0:T(8,128)(2,1)}), bf16[4,128,512]{2,1,0:T(8,128)(2,1)S(1)}, u32[]{:S(2)}, u32[]{:S(2)}) %all-to-all-start.2) | async-done | bytes 524320 | tf_op jit(solution)/shard_map/all_to_all | solution.py:35
  192.9 0.1 multiply_convert_fusion
  193.0 65.0 %all-gather.5.cloned.1.call-done = bf16[4,512,512]{2,1,0:T(8,128)(2,1)} async-done(((bf16[4,8,512]{2,1,0:T(8,128)(2,1)}), bf16[4,512,512]{2,1,0:T(8,128)(2,1)}) %all-gather.5.cloned.1.call-update) | async-done | bytes 2097168 | tf_op jit(solution)/shard_map/all_gather | solution.py:101
  258.0 3.6 %gather_fusion.1 = bf16[64,4,8,512]{3,2,1,0:T(8,128)(2,1)} fusion(bf16[4,64,8,512]{3,2,1,0:T(8,128)(2,1)} %bitcast.79, s32[1024]{0:T(1024)S(1)} %pad_clamp_fusion), kind=kCustom, calls=%fused_computation.1 | custom fusion | bytes 4194560 | tf_op jit(solution)/shard_map/gather | solution.py:106
  261.6 0.0 copy-done.3
  261.6 5.5 %fusion.9 = bf16[512,4,512]{0,2,1:T(8,128)(2,1)} fusion(bf16[512,512,1]{1,0,2:T(8,128)(2,1)S(1)} %bitcast.82, f32[4]{0:T(128)S(1)} %get-tuple-element.17, bf16[64,4,8,512]{3,2,1,0:T(8,128)(2,1)S(1)} %bitcast.78, bf16[64,4,8,512]{3,2,1,0:T(8,128)(2,1)} %gather_fusion.1), kind=kOutput, calls=%fused_computation.15 | convolution fusion | flops 2152726528 | bytes 6815760 | tf_op jit(solution)/shard_map/dot_general | solution.py:114
  267.1 3.9 %copy.29 = bf16[512,2048]{1,0:T(8,128)(2,1)} copy(bf16[512,2048]{0,1:T(8,128)(2,1)} %bitcast.80) | data formatting | bytes 4194304
  (9 shorter events, 0.1 us)
Async XLA Ops:
  7.2 3.6 %copy-start.5 = (s32[64]{0:T(128)S(1)}, s32[64]{0:T(128)}, u32[]{:S(2)}) copy-start(s32[64]{0:T(128)} %param.11) | copy-start | bytes 772
  12.8 95.5 %all-to-all-start.3 = ((bf16[64,4,8,512]{3,2,1,0:T(8,128)(2,1)}), bf16[64,4,8,512]{3,2,1,0:T(8,128)(2,1)S(1)}, u32[]{:S(2)}, u32[]{:S(2)}) async-start(bf16[64,4,8,512]{3,2,1,0:T(8,128)(2,1)} %gather_fusion), calls=%async_computation.3 | async-start | bytes 4194304 | tf_op jit(solution)/shard_map/all_to_all | solution.py:29
  27.0 81.3 %copy-start.4 = (s32[4]{0:T(128)S(1)}, s32[4]{0:T(128)}, u32[]{:S(2)}) copy-start(s32[4]{0:T(128)} %param.10) | copy-start | bytes 52
  27.0 118.1 %all-gather.3.cloned.1.call-start = ((), (), s32[]{:S(2)}) async-start(), calls=%async_computation.4 | async-start | bytes 2129920 | tf_op jit(solution)/shard_map/all_gather | solution.py:93
  27.7 230.3 %all-gather.5.cloned.1.call-start = ((), (), s32[]{:S(2)}) async-start(), calls=%async_computation.5 | async-start | bytes 2129920 | tf_op jit(solution)/shard_map/all_gather | solution.py:101
  145.1 2.7 copy-start
  149.7 2.5 copy-start.1
  152.2 12.6 %copy-start.2 = (bf16[1,128,512]{2,1,0:T(8,128)(2,1)S(1)}, bf16[1,128,512]{2,1,0:T(8,128)(2,1)}, u32[]{:S(2)}) copy-start(bf16[1,128,512]{2,1,0:T(8,128)(2,1)} %param.7) | copy-start | bytes 393220
  165.6 12.3 %all-to-all-start.1 = ((bf16[4,128,512]{2,1,0:T(8,128)(2,1)}), bf16[4,128,512]{2,1,0:T(8,128)(2,1)S(1)}, u32[]{:S(2)}, u32[]{:S(2)}) async-start(bf16[4,128,512]{2,1,0:T(8,128)(2,1)} %broadcast_in_dim.97), calls=%async_computation.1 | async-start | bytes 1048576 | tf_op jit(solution)/shard_map/all_to_all | solution.py:35
  179.8 81.8 %copy-start.3 = (bf16[128,512]{1,0:T(8,128)(2,1)}, bf16[128,512]{1,0:T(8,128)(2,1)S(1)}, u32[]{:S(2)}) copy-start(bf16[128,512]{1,0:T(8,128)(2,1)S(1)} %fusion.23) | copy-start | bytes 393220
  180.6 12.3 %all-to-all-start.2 = ((bf16[4,128,512]{2,1,0:T(8,128)(2,1)}), bf16[4,128,512]{2,1,0:T(8,128)(2,1)S(1)}, u32[]{:S(2)}, u32[]{:S(2)}) async-start(bf16[4,128,512]{2,1,0:T(8,128)(2,1)} %broadcast_in_dim.98), calls=%async_computation.2 | async-start | bytes 1048576 | tf_op jit(solution)/shard_map/all_to_all | solution.py:35
Sparse Core Ops, SparseCore 0:
  31.3 113.8 all-gather.2
  152.3 105.6 all-gather.4
where the time goes:
time: 279 us; the launch traced here: 278 us
  waiting for transfers between devices  118 us (42%)
  blocking collectives  87.5 us (31%)
  starting transfers between devices  21.4 us (8%)
  matrix products  19.2 us (7%)
  between operations  16.3 us (6%)
  local copies, waits for them, and re-layouts  11.8 us (4%)
  other arithmetic  3.55 us (1%)
    psum x5, blocking collectives, over_axes(): x = lax.psum(x, axis)  76.2 us
    all_gather x1, waiting for transfers between devices, shards(): lax.all_gather(right_code, GROUP, axis=1, tiled=True)  65 us
    all_gather x1, waiting for transfers between devices, shards(): lax.all_gather(prev_right, GROUP, axis=1, tiled=True).astype(jnp.float32)  36.5 us
    all_to_all x2, waiting for transfers between devices, from_everyone(): return lax.all_to_all(copies, axis, split_axis=0, concat_axis=0, tiled=True)  15.8 us
    all_to_all x1, starting transfers between devices, sent_and_summed(): lax.all_to_all(pieces, axis, split_axis=0, concat_axis=0, tiled=True)  14.2 us
    all_to_all x1, blocking collectives, sent_and_summed(): lax.all_to_all(pieces, axis, split_axis=0, concat_axis=0, tiled=True)  11.3 us
    dot_general x10, matrix products, newton_rows(): product = jnp.matmul(product, start_root, precision=lax.Precision.HIGHEST)  8.9 us
    all_to_all x2, starting transfers between devices, from_everyone(): return lax.all_to_all(copies, axis, split_axis=0, concat_axis=0, tiled=True)  7.12 us
  transfers between devices with their start and end apart: 5, of which 4 were waited for; matrix products, arithmetic and copies ran while one was open for 3% of the time, Pallas kernels for 0%

commit v1 on v0

v1 whole, which is shorter than its diff:
```python
import functools

import jax
import jax.numpy as jnp
from jax import lax
from jax.experimental import pallas as pl
from jax.experimental.pallas import tpu as pltpu
from jax.sharding import Mesh
from jax.sharding import PartitionSpec as P

AXES = ("z", "yh", "x", "yl", "c")
GROUP = ("z", "yh", "x")
REPLICA = ("yl", "c")
MESH_ID = pl.DeviceIdType.MESH
F32 = jnp.float32
BF16 = jnp.bfloat16

EPSILON = 1e-06
B = 512
CUT = 384
ROUNDS = 4
PLANE = ((0, 1), (1, 0), (0, 3), (0, 2), (1, 1), (1, 3), (1, 2))
DEPTH = (1, 7, 2, 6, 3, 5, 4)


def pow_two(exponent):
    result = jnp.float32(0.0)
    for power in range(-4, 5):
        result = result + jnp.where(exponent == power, jnp.float32(2.0**power), jnp.float32(0.0))
    return result


def five_products(rows, root):
    count = rows.shape[0]
    for repeat in range(5):
        high = rows.astype(BF16)
        low = (rows - high.astype(F32)).astype(BF16)
        both = jnp.dot(jnp.concatenate([high, low], axis=0), root, preferred_element_type=F32)
        rows = both[:count] + both[count:]
    return rows


def exchange_kernel(
    exp_left, exp_right, owner_of, grad, prev_left, prev_right,
    middle, left_all, left_own, right_own,
    gram, plane_in, depth_in, plane_sum, depth_sum, strip_z, strip_p,
    norm_own, norm_mid, norm_p, norm_z,
    xz, xp, root, code,
    lgram, lin1, lsend, lin2, lroot, lcode, lnorm, lnorm_in,
    sem_plane, sem_depth, sem_sz, sem_sp, sem_n1, sem_n2, sem_xz, sem_xp,
    sem_cz, sem_cp, sem_fp, sem_fz, sem_l,
):
    z, yh, x = lax.axis_index("z"), lax.axis_index("yh"), lax.axis_index("x")
    yl, c = lax.axis_index("yl"), lax.axis_index("c")
    p = yh * 4 + x
    me_r = p // 2

    def plane_peer(step):
        return ((yh + step[0]) % 2, (x + step[1]) % 4)

    def plane_id(step):
        a, b = plane_peer(step)
        return (z, a, b, yl, c)

    def depth_id(step):
        return ((z + step) % 8, yh, x, yl, c)

    core_id = (z, yh, x, yl, 1 - c)
    side_id = (z, yh, x, 1 - yl, c)

    def send(src, dst, sems, device):
        copy = pltpu.make_async_remote_copy(
            src_ref=src, dst_ref=dst, send_sem=sems[0], recv_sem=sems[1],
            device_id=device, device_id_type=MESH_ID,
        )
        copy.start()
        return copy

    def two(sem, *index):
        return sem.at[(0, *index)], sem.at[(1, *index)]

    pending = []

    barrier = pltpu.get_barrier_semaphore()
    for step in PLANE:
        pl.semaphore_signal(barrier, inc=1, device_id=plane_id(step), device_id_type=MESH_ID)
    for step in DEPTH:
        pl.semaphore_signal(barrier, inc=1, device_id=depth_id(step), device_id_type=MESH_ID)
    for device in (core_id, side_id):
        pl.semaphore_signal(barrier, inc=1, device_id=device, device_id_type=MESH_ID)

    tile_row = lax.broadcasted_iota(jnp.int32, (128, 128), 0)
    tile_col = lax.broadcasted_iota(jnp.int32, (128, 128), 1)
    norm_row = lax.broadcasted_iota(jnp.int32, (8, 128), 0)

    def right_gram(r, norms):
        piece = grad[:, pl.ds(pl.multiple_of(r * B, B), B)]
        part = lax.dot_general(piece, piece, (((0,), (0,)), ((), ())), preferred_element_type=F32)
        diag = jnp.zeros((128, 128), F32)
        for k in range(4):
            square = part[k * 128 : (k + 1) * 128, k * 128 : (k + 1) * 128]
            diag = diag + jnp.where(tile_row == tile_col, square, 0.0)
        lanes = jnp.sum(diag, axis=0, keepdims=True)
        gram[pl.ds(2 * r, 2)] = part.astype(BF16).reshape(2, 8, 32, B)
        return norms + jnp.where(norm_row == r, jnp.broadcast_to(lanes, (8, 128)), 0.0)

    norms = lax.fori_loop(0, 4, right_gram, jnp.zeros((8, 128), F32))
    norm_own[...] = norms
    lnorm[...] = norms
    xz[z] = prev_right[...]
    lroot[yl, c] = prev_left[0]

    pl.semaphore_wait(barrier, len(PLANE) + len(DEPTH) + 2)

    x_depth = [
        send(prev_right, xz.at[z], two(sem_xz, k), depth_id(step)) for k, step in enumerate(DEPTH)
    ]
    lx_core = send(prev_left.at[0], lroot.at[yl, c], two(sem_l, 0), core_id)
    lx_side = send(prev_left.at[0], lroot.at[yl, c], two(sem_l, 1), side_id)
    first = []
    for j, turn in enumerate((2, 1, 3, 0)):
        zz = ((z // 2 + turn) % 4) * 2
        rr = ((me_r + turn) % 4) * 2
        sent = []
        for k in range(7):
            a, b = plane_peer(PLANE[k])
            sent.append(
                send(
                    gram.at[a * 4 + b, pl.ds(zz, 2), :, pl.ds(0, CUT)], plane_in.at[k, j],
                    two(sem_plane, j, k), plane_id(PLANE[k]),
                )
            )
            sent.append(
                send(
                    gram.at[pl.ds(rr, 2), (z + DEPTH[k]) % 8, :, pl.ds(CUT, B - CUT)],
                    depth_in.at[k, j], two(sem_depth, j, k), depth_id(DEPTH[k]),
                )
            )
        first.append((zz, rr, sent))
        if j == 0:
            n_first = [
                send(norm_own, norm_p.at[k], two(sem_n1, k), plane_id(step))
                for k, step in enumerate(PLANE)
            ]
            n_core = send(lnorm, lnorm_in.at[0], two(sem_l, 2), core_id)

    def left_gram(i, carry):
        rows = grad[pl.ds(pl.multiple_of(i * 128, 128), 128), :]
        part = lax.dot_general(rows, grad[...], (((1,), (1,)), ((), ())), preferred_element_type=F32)
        lgram[i // 2, i % 2] = part.astype(BF16)
        return carry

    lax.fori_loop(0, 4, left_gram, 0)
    l_core = send(lgram.at[:, 1 - c], lin1, two(sem_l, 3), core_id)

    lx_side.wait_recv()
    lx_pass = send(lroot.at[1 - yl, c], lroot.at[1 - yl, c], two(sem_l, 4), core_id)
    n_core.wait()
    lnorm[...] = lnorm[...] + lnorm_in[0]
    n_side = send(lnorm, lnorm_in.at[1], two(sem_l, 5), side_id)

    for copy in x_depth:
        copy.wait_recv()
    xp[p] = xz[:, me_r]
    x_plane = []
    for k, step in enumerate(PLANE):
        a, b = plane_peer(step)
        x_plane.append(send(xz.at[:, (a * 4 + b) // 2], xp.at[p], two(sem_xp, k), plane_id(step)))

    l_core.wait_recv()
    lsum = lgram[:, c].astype(F32) + lin1[...].astype(F32)
    lsend[...] = lsum.astype(BF16)
    l_side = send(lsend.at[1 - yl], lin2, two(sem_l, 6), side_id)

    for copy in n_first:
        copy.wait_recv()
    total = norm_own[...]
    for k in range(7):
        total = total + norm_p[k]
    norm_mid[...] = total
    n_second = [
        send(norm_mid, norm_z.at[k], two(sem_n2, k), depth_id(step)) for k, step in enumerate(DEPTH)
    ]

    lx_core.wait_recv()
    lx_pass.wait_recv()
    n_side.wait()
    l_side.wait_recv()
    left_scale = jnp.sum(jnp.where(norm_row < 4, lnorm[...] + lnorm_in[1], 0.0)) / B + EPSILON
    left_rows = lsend[yl].astype(F32) + lin2[...].astype(F32)
    product = five_products(left_rows, lroot[...].reshape(B, B)) / left_scale
    left_new = (5.0 * prev_left[0].astype(F32) - product) / 4.0
    left_code = (left_new * pow_two(-exp_left[0])).astype(BF16)
    left_own[...] = left_code

    second = []
    for j in range(ROUNDS):
        zz, rr, sent = first[j]
        for copy in sent:
            copy.wait_recv()
        acc = gram[p, pl.ds(zz, 2), :, pl.ds(0, CUT)].astype(F32)
        for k in range(7):
            acc = acc + plane_in[k, j].astype(F32)
        plane_sum[j] = acc.astype(BF16)
        acc = gram[pl.ds(rr, 2), z, :, pl.ds(CUT, B - CUT)].astype(F32)
        for k in range(7):
            acc = acc + depth_in[k, j].astype(F32)
        depth_sum[j] = acc.astype(BF16)
        if j < ROUNDS - 1:
            for b in range(2):
                second.append(
                    send(plane_sum.at[j, b], strip_z.at[z], (sem_sz.at[0, 2 * j + b], sem_sz.at[1, z]),
                         (zz + b, yh, x, yl, c))
                )
                q = rr + b
                second.append(
                    send(depth_sum.at[j, b], strip_p.at[p], (sem_sp.at[0, 2 * j + b], sem_sp.at[1, p]),
                         (z, q // 4, q % 4, yl, c))
                )
        else:
            b = 1 - z % 2
            second.append(
                send(plane_sum.at[j, b], strip_z.at[z], (sem_sz.at[0, 6], sem_sz.at[1, z]),
                     (zz + b, yh, x, yl, c))
            )
            b = 1 - p % 2
            q = rr + b
            second.append(
                send(depth_sum.at[j, b], strip_p.at[p], (sem_sp.at[0, 6], sem_sp.at[1, p]),
                     (z, q // 4, q % 4, yl, c))
            )
    strip_z[z] = plane_sum[ROUNDS - 1, z % 2]
    strip_p[p] = depth_sum[ROUNDS - 1, p % 2]

    for copy in x_plane:
        copy.wait_recv()

    def lay(i, carry):
        rows = xp[:, i].astype(F32).reshape(64, B).astype(BF16)
        root[pl.ds(pl.multiple_of(i * 64, 64), 64), :] = rows
        return carry

    lax.fori_loop(0, 8, lay, 0)

    for copy in n_second:
        copy.wait_recv()
    total = norm_mid[...]
    for k in range(7):
        total = total + norm_z[k]
    right_scale = jnp.sum(jnp.where(norm_row == me_r, total, 0.0)) / B + EPSILON

    def arrived(buffer, sems, index):
        pltpu.make_async_remote_copy(
            src_ref=buffer.at[index], dst_ref=buffer.at[index], send_sem=sems.at[0, 0],
            recv_sem=sems.at[1, index], device_id=core_id, device_id_type=MESH_ID,
        ).wait_recv()

    for step in range(1, 8):
        arrived(strip_z, sem_sz, (z + step) % 8)
        arrived(strip_p, sem_sp, (p + step) % 8)
    acc_a = strip_z[0].astype(F32)
    acc_b = strip_p[0].astype(F32)
    for k in range(1, 8):
        acc_a = acc_a + strip_z[k].astype(F32)
        acc_b = acc_b + strip_p[k].astype(F32)
    rows = jnp.concatenate([acc_a, acc_b], axis=1)
    product = five_products(rows, root[...]) / right_scale
    start = root[pl.ds(pl.multiple_of((p % 2) * 256 + z * 32, 32), 32), :].astype(F32)
    right_new = (5.0 * start - product) / 4.0
    code[p, z] = (right_new * pow_two(-exp_right[me_r])).astype(BF16)

    to_depth = [
        send(code.at[p, z, :, pl.ds(0, CUT)], code.at[p, z, :, pl.ds(0, CUT)],
             two(sem_cz, k), depth_id(step))
        for k, step in enumerate(DEPTH)
    ]
    to_plane = [
        send(code.at[p, z], code.at[p, z], two(sem_cp, k), plane_id(step))
        for k, step in enumerate(PLANE)
    ]
    left_all[yl, c] = left_own[...]
    lc_core = send(left_own, lcode.at[yl, c], two(sem_l, 7), core_id)
    lc_side = send(left_own, lcode.at[yl, c], two(sem_l, 8), side_id)

    on_plane = []
    for i, dz in enumerate(DEPTH):
        to_depth[i].wait_recv()
        other = (z + 8 - dz) % 8
        for k, step in enumerate(PLANE):
            on_plane.append(
                send(code.at[p, other, :, pl.ds(0, CUT)], code.at[p, other, :, pl.ds(0, CUT)],
                     two(sem_fp, i, k), plane_id(step))
            )
    for copy in to_plane:
        copy.wait_recv()
    on_depth = [
        send(code.at[:, z, :, pl.ds(CUT, B - CUT)], code.at[:, z, :, pl.ds(CUT, B - CUT)],
             two(sem_fz, k), depth_id(step))
        for k, step in enumerate(DEPTH)
    ]
    lc_side.wait_recv()
    lc_pass = send(lcode.at[1 - yl, c], lcode.at[1 - yl, c], two(sem_l, 9), core_id)
    lc_core.wait_recv()
    lc_pass.wait_recv()
    left_all[yl, 1 - c] = lcode[yl, 1 - c]
    left_all[1 - yl] = lcode[1 - yl]
    for copy in on_plane:
        copy.wait_recv()
    for copy in on_depth:
        copy.wait_recv()

    owned = owner_of[z * 8 + p]
    for r in range(4):
        strip = code[2 * r + owned // 32, (owned // 4) % 8].astype(F32)
        picked = jnp.zeros((8, B), F32)
        for k in range(4):
            picked = picked + jnp.where(owned % 4 == k, strip[8 * k : 8 * k + 8], 0.0)
        right_own[r] = picked.astype(BF16)

    def mix(r, carry):
        columns = pl.ds(pl.multiple_of(r * B, B), B)
        full = code[pl.ds(2 * r, 2)].reshape(B, B)
        out = jnp.dot(grad[:, columns], full, preferred_element_type=F32)
        middle[:, columns] = (out * pow_two(exp_right[r])).astype(BF16)
        return carry

    lax.fori_loop(0, 4, mix, 0)

    for _, _, sent in first:
        for copy in sent:
            copy.wait_send()
    for copy in (
        x_depth + x_plane + n_first + n_second + second + to_depth + to_plane + on_plane + on_depth
        + [lx_core, lx_side, lx_pass, l_core, l_side, lc_core, lc_side, lc_pass]
    ):
        copy.wait_send()


def final_kernel(exp_left, left_all, middle, left_code, right_code, precond, root_left, root_right):
    out = jnp.dot(left_all[...], middle[...], preferred_element_type=F32)
    precond[...] = (out * pow_two(exp_left[0])).astype(BF16)
    root_left[0] = left_code[...]
    root_right[:, 0] = right_code[...]


def shards(grad, prev_left, prev_right, exp_left, exp_right, strip_owner):
    smem = pl.BlockSpec(memory_space=pltpu.SMEM)
    vmem = pl.BlockSpec(memory_space=pltpu.VMEM)
    dma = pltpu.SemaphoreType.DMA
    shape = jax.ShapeDtypeStruct
    middle, left_all, left_own, right_own = pl.pallas_call(
        exchange_kernel,
        out_shape=(
            shape((B, 4 * B), BF16), shape((2, 2, 128, B), BF16), shape((128, B), BF16),
            shape((4, 8, B), BF16),
        ),
        in_specs=[smem, smem, smem, vmem, vmem, vmem],
        out_specs=(vmem,) * 4,
        scratch_shapes=[
            pltpu.VMEM((8, 8, 32, B), BF16),
            pltpu.VMEM((7, ROUNDS, 2, 32, CUT), BF16),
            pltpu.VMEM((7, ROUNDS, 2, 32, B - CUT), BF16),
            pltpu.VMEM((ROUNDS, 2, 32, CUT), BF16),
            pltpu.VMEM((ROUNDS, 2, 32, B - CUT), BF16),
            pltpu.VMEM((8, 32, CUT), BF16),
            pltpu.VMEM((8, 32, B - CUT), BF16),
            pltpu.VMEM((8, 128), F32),
            pltpu.VMEM((8, 128), F32),
            pltpu.VMEM((7, 8, 128), F32),
            pltpu.VMEM((7, 8, 128), F32),
            pltpu.VMEM((8, 4, 8, B), BF16),
            pltpu.VMEM((8, 8, 8, B), BF16),
            pltpu.VMEM((B, B), BF16),
            pltpu.VMEM((8, 8, 32, B), BF16),
            pltpu.VMEM((2, 2, 128, B), BF16),
            pltpu.VMEM((2, 128, B), BF16),
            pltpu.VMEM((2, 128, B), BF16),
            pltpu.VMEM((128, B), BF16),
            pltpu.VMEM((2, 2, 128, B), BF16),
            pltpu.VMEM((2, 2, 128, B), BF16),
            pltpu.VMEM((8, 128), F32),
            pltpu.VMEM((2, 8, 128), F32),
            dma((2, ROUNDS, 7)), dma((2, ROUNDS, 7)), dma((2, 8)), dma((2, 8)),
            dma((2, 7)), dma((2, 7)), dma((2, 7)), dma((2, 7)),
            dma((2, 7)), dma((2, 7)), dma((2, 7, 7)), dma((2, 7)), dma((2, 10)),
        ],
        compiler_params=pltpu.CompilerParams(
            collective_id=0, has_side_effects=True, vmem_limit_bytes=40 << 20
        ),
        name="exchange",
    )(exp_left, exp_right, strip_owner, grad, prev_left, prev_right)
    return pl.pallas_call(
        final_kernel,
        grid=(4,),
        out_shape=(
            shape((B, 4 * B), BF16), shape((1, 128, B), BF16), shape((4, 1, 8, B), BF16),
        ),
        in_specs=[
            smem,
            pl.BlockSpec((B, B), lambda i: (0, 0)),
            pl.BlockSpec((B, B), lambda i: (0, i)),
            pl.BlockSpec((128, B), lambda i: (0, 0)),
            pl.BlockSpec((4, 8, B), lambda i: (0, 0, 0)),
        ],
        out_specs=(
            pl.BlockSpec((B, B), lambda i: (0, i)),
            pl.BlockSpec((1, 128, B), lambda i: (0, 0, 0)),
            pl.BlockSpec((4, 1, 8, B), lambda i: (0, 0, 0, 0)),
        ),
        name="final",
    )(exp_left, left_all.reshape(B, B), middle, left_own, right_own)


def solution(mesh):
    torus = Mesh(mesh.devices.reshape(8, 2, 4, 2, 2), AXES)
    in_specs = (
        P(GROUP, REPLICA),
        P(GROUP, REPLICA, None),
        P(REPLICA, GROUP, None),
        P(GROUP),
        P(REPLICA),
        P(),
    )
    out_specs = (P(GROUP, REPLICA), P(GROUP, REPLICA, None), P(REPLICA, GROUP, None, None))
    return jax.shard_map(
        shards, mesh=torus, in_specs=in_specs, out_specs=out_specs, check_vma=False
    )
```

time: 279 us -> 89 us (0.32)
  waiting for transfers between devices: 118 us -> 0 us
  blocking collectives: 87.5 us -> 0 us
  Pallas kernels: 0 us -> 79.4 us
  starting transfers between devices: 21.4 us -> 0 us
  matrix products: 19.2 us -> 0 us
  between operations: 16.3 us -> 1.31 us
  local copies, waits for them, and re-layouts: 11.8 us -> 7.95 us
  other arithmetic: 3.55 us -> 0 us
    all_gather x2 -> x0, waiting for transfers between devices: 102 us -> none  [the longest x1 65 us: shards(): lax.all_gather(right_code, GROUP, axis=1, tiled=True)]
    pallas_call x0 -> x2, Pallas kernels: none -> 79.4 us  [the longest x1 74.6 us: shards(): pl.pallas_call(exchange_kernel, out_shape=(shape((B, 4 * B), BF16), shape...]
    psum x5 -> x0, blocking collectives: 76.2 us -> none  [over_axes(): x = lax.psum(x, axis)]
    all_to_all x3 -> x0, starting transfers between devices: 21.3 us -> none  [the longest x1 14.2 us: sent_and_summed(): lax.all_to_all(pieces, axis, split_axis=0, concat_axis=0, tiled=True)]
    dot_general x13 -> x0, matrix products: 19.2 us -> none  [the longest x10 8.9 us: newton_rows(): product = jnp.matmul(product, start_root, precision=lax.Precision.HIGHEST)]
    all_to_all x3 -> x0, waiting for transfers between devices: 15.8 us -> none  [the longest x2 15.8 us: from_everyone(): return lax.all_to_all(copies, axis, split_axis=0, concat_axis=0, tiled=True)]
    all_to_all x1 -> x0, blocking collectives: 11.3 us -> none  [sent_and_summed(): lax.all_to_all(pieces, axis, split_axis=0, concat_axis=0, tiled=True)]
    gather x2 -> x0, local copies, waits for them, and re-layouts: 5.59 us -> none  [the longest x1 3.59 us: shards(): right_owned[:, inverse].reshape(col_count, block_size, block_size)]
  transfers between devices with their start and end apart: 5 -> 0, of which waited for: 4 -> 0; matrix products, arithmetic and copies ran while one was open for 3% -> 0% of each run, Pallas kernels for 0% -> 0%
where the time goes in v1:
time: 89 us; the launch traced here: 88.7 us
  Pallas kernels  79.4 us (89%)
  local copies, waits for them, and re-layouts  7.95 us (9%)
  between operations  1.31 us (1%)
    pallas_call x1, Pallas kernels, shards(): pl.pallas_call(exchange_kernel, out_shape=(shape((B, 4 * B), BF16), shape...  74.6 us
    unnamed x18, local copies, waits for them, and re-layouts  7.95 us
    pallas_call x1, Pallas kernels, shards(): pl.pallas_call(final_kernel, grid=(4,), out_shape=(shape((B, 4 * B), BF16...  4.77 us

profile of v1, /device:TPU:32, one launch (start us, length us, event | category | flops | bytes accessed | tf_op | source)
XLA Modules:
  0.0 88.7 jit_solution(13232462871768397838)
XLA Ops:
  1.3 0.0 copy-start
  1.3 1.6 %copy-done = bf16[512,2048]{1,0:T(8,128)(2,1)S(1)} copy-done((bf16[512,2048]{1,0:T(8,128)(2,1)S(1)}, bf16[512,2048]{1,0:T(8,128)(2,1)}, u32[]{:S(2)}) %copy-start) | copy-done | bytes 2097176
  2.9 0.0 copy-start.3
  2.9 0.9 %copy-done.3 = bf16[1,128,512]{2,1,0:T(8,128)(2,1)S(1)} copy-done((bf16[1,128,512]{2,1,0:T(8,128)(2,1)S(1)}, bf16[1,128,512]{2,1,0:T(8,128)(2,1)}, u32[]{:S(2)}) %copy-start.3) | copy-done | bytes 131096
  3.8 0.0 copy-start.5
  3.8 0.8 copy-done.5
  4.5 0.0 copy-start.7
  4.5 0.7 copy-done.7
  5.2 0.0 copy-start.8
  5.2 0.7 copy-done.8
  5.8 74.6 %exchange.1 = (bf16[512,2048]{1,0:T(8,128)(2,1)S(1)}, bf16[2,2,128,512]{3,2,1,0:T(8,128)(2,1)S(1)}, bf16[128,512]{1,0:T(8,128)(2,1)S(1)}, bf16[4,8,512]{2,1,0:T(8,128)(2,1)S(1)}) custom-call(s32[1]{0:T(128)S(6)} %copy.9.exp_left, s32[4]{0:T(128)S(1)} %copy-done.7, s32[64]{0:T(128)S(1)} %copy-done.8, bf16[512,2048]{1,0:T(8,128)(2,1)S(1)} %copy-done, ...), custom_call_target="tpu_custom_call" | custom-call | tf_op jit(solution)/shard_map/exchange/pallas_call | solution.py:351
  80.5 0.0 copy-start.1
  80.5 1.3 %copy-done.1 = bf16[512,2048]{1,0:T(8,128)(2,1)} copy-done((bf16[512,2048]{1,0:T(8,128)(2,1)}, bf16[512,2048]{1,0:T(8,128)(2,1)S(1)}, u32[]{:S(2)}) %copy-start.1) | copy-done | bytes 2097176
  81.8 0.0 copy-start.2
  81.8 0.8 copy-done.2
  82.6 0.0 copy-start.4
  82.6 0.7 copy-done.4
  83.3 0.0 copy-start.6
  83.3 0.6 copy-done.6
  83.9 4.8 %final.1 = (bf16[512,2048]{1,0:T(8,128)(2,1)}, bf16[1,128,512]{2,1,0:T(8,128)(2,1)}, bf16[4,1,8,512]{3,2,1,0:T(8,128)(2,1)}) custom-call(s32[1]{0:T(128)S(6)} %copy.9.exp_left, bf16[512,512]{1,0:T(8,128)(2,1)} %bitcast.1, bf16[512,2048]{1,0:T(8,128)(2,1)} %copy-done.1, bf16[128,512]{1,0:T(8,128)(2,1)} %copy-done.4, bf16[4,8,512]{2,1,0:T(8,128)(2,1)} %copy-done.6), custom_call_target="tpu_custom_call" | custom-call | tf_op jit(solution)/shard_map/final/pallas_call | solution.py:392
Async XLA Ops:
  1.3 1.6 %copy-start = (bf16[512,2048]{1,0:T(8,128)(2,1)S(1)}, bf16[512,2048]{1,0:T(8,128)(2,1)}, u32[]{:S(2)}) copy-start(bf16[512,2048]{1,0:T(8,128)(2,1)} %grad.1) | copy-start | bytes 6291460
  2.9 0.9 %copy-start.3 = (bf16[1,128,512]{2,1,0:T(8,128)(2,1)S(1)}, bf16[1,128,512]{2,1,0:T(8,128)(2,1)}, u32[]{:S(2)}) copy-start(bf16[1,128,512]{2,1,0:T(8,128)(2,1)} %prev_left.1) | copy-start | bytes 393220
  3.8 0.8 copy-start.5
  4.5 0.7 copy-start.7
  5.2 0.7 copy-start.8
  80.5 1.3 %copy-start.1 = (bf16[512,2048]{1,0:T(8,128)(2,1)}, bf16[512,2048]{1,0:T(8,128)(2,1)S(1)}, u32[]{:S(2)}) copy-start(bf16[512,2048]{1,0:T(8,128)(2,1)S(1)} %get-tuple-element.8.middle) | copy-start | bytes 6291460
  81.8 0.8 copy-start.2
  82.6 0.7 copy-start.4
  83.3 0.6 copy-start.6

commit v2 on v1

v2 whole, which is shorter than its diff:
```python
import contextlib

import jax
import jax.numpy as jnp
from jax import lax
from jax.experimental import pallas as pl
from jax.experimental.pallas import tpu as pltpu
from jax.sharding import Mesh
from jax.sharding import PartitionSpec as P

AXES = ("z", "yh", "x", "yl", "c")
GROUP = ("z", "yh", "x")
REPLICA = ("yl", "c")
MESH_ID = pl.DeviceIdType.MESH
F32 = jnp.float32
BF16 = jnp.bfloat16

EPSILON = 1e-06
B = 512
CUT = 384
ROUNDS = 4
PLANE = ((0, 1), (1, 0), (0, 3), (0, 2), (1, 1), (1, 3), (1, 2))
ROW = ((0, 1), (0, 3), (0, 2))
DEPTH = (1, 7, 2, 6, 3, 5, 4)


def pow_two(exponent):
    result = jnp.float32(0.0)
    for power in range(-4, 5):
        result = result + jnp.where(exponent == power, jnp.float32(2.0**power), jnp.float32(0.0))
    return result


def five_products(rows, root):
    count = rows.shape[0]
    for repeat in range(5):
        high = rows.astype(BF16)
        low = (rows - high.astype(F32)).astype(BF16)
        both = jnp.dot(jnp.concatenate([high, low], axis=0), root, preferred_element_type=F32)
        rows = both[:count] + both[count:]
    return rows


def exchange_kernel(
    exp_left_in, exp_right_in, owner_in, grad_in, prev_left_in, prev_right_in,
    middle_out, left_out, right_out,
    exp_left, exp_right, owner_of, grad, prev_left, prev_right,
    middle, left_own, right_own,
    gram_d, gram_o, plane_in, depth_in, plane_sum, depth_sum, strip_z, strip_p,
    turned, miss_a, miss_b,
    norm_own, norm_mid, norm_p, norm_z,
    xz, x_across, xp, root, code,
    lgram, lin1, lsend, lin2, lroot, lcode, lnorm, lnorm_in,
    sent, got, got_plane, got_depth, got_strip, got_pass, sem_l, sem_in,
):
    z, yh, x = lax.axis_index("z"), lax.axis_index("yh"), lax.axis_index("x")
    yl, c = lax.axis_index("yl"), lax.axis_index("c")
    p = yh * 4 + x
    across = (1 - yh) * 4 + x
    me_r = p // 2

    def plane_peer(step):
        return ((yh + step[0]) % 2, (x + step[1]) % 4)

    def plane_id(step):
        a, b = plane_peer(step)
        return (z, a, b, yl, c)

    def depth_id(step):
        return ((z + step) % 8, yh, x, yl, c)

    core_id = (z, yh, x, yl, 1 - c)
    side_id = (z, yh, x, 1 - yl, c)

    def send(src, dst, sems, device):
        copy = pltpu.make_async_remote_copy(
            src_ref=src, dst_ref=dst, send_sem=sems[0], recv_sem=sems[1],
            device_id=device, device_id_type=MESH_ID,
        )
        copy.start()
        return copy

    def two(sem, *index):
        return sem.at[(0, *index)], sem.at[(1, *index)]

    def all_sent(ref, sem):
        pltpu.make_async_remote_copy(
            src_ref=ref, dst_ref=ref, send_sem=sem, recv_sem=sem,
            device_id=core_id, device_id_type=MESH_ID,
        ).wait_send()

    def all_here(ref, sem):
        pltpu.make_async_remote_copy(
            src_ref=ref, dst_ref=ref, send_sem=sem, recv_sem=sem,
            device_id=core_id, device_id_type=MESH_ID,
        ).wait_recv()

    def fetch(src, dst, index):
        copy = pltpu.make_async_copy(src, dst, sem_in.at[index])
        copy.start()
        return copy

    get_right = fetch(prev_right_in, prev_right, 0)
    get_grad = [
        fetch(grad_in.at[:, pl.ds(r * B, B)], grad.at[:, pl.ds(r * B, B)], 1 + r) for r in range(4)
    ]
    get_rest = [
        fetch(prev_left_in, prev_left, 5), fetch(exp_left_in, exp_left, 6),
        fetch(exp_right_in, exp_right, 7), fetch(owner_in, owner_of, 8),
    ]

    barrier = pltpu.get_barrier_semaphore()
    for step in PLANE:
        pl.semaphore_signal(barrier, inc=1, device_id=plane_id(step), device_id_type=MESH_ID)
    for step in DEPTH:
        pl.semaphore_signal(barrier, inc=1, device_id=depth_id(step), device_id_type=MESH_ID)
    for device in (core_id, side_id):
        pl.semaphore_signal(barrier, inc=1, device_id=device, device_id_type=MESH_ID)

    tile_row = lax.broadcasted_iota(jnp.int32, (128, 128), 0)
    tile_col = lax.broadcasted_iota(jnp.int32, (128, 128), 1)
    norm_row = lax.broadcasted_iota(jnp.int32, (8, 128), 0)

    def right_gram(r, norms):
        pltpu.make_async_copy(
            grad_in.at[:, pl.ds(pl.multiple_of(r * B, B), B)],
            grad.at[:, pl.ds(pl.multiple_of(r * B, B), B)], sem_in.at[1 + r],
        ).wait()
        piece = grad[:, pl.ds(pl.multiple_of(r * B, B), B)]
        part = lax.dot_general(piece, piece, (((0,), (0,)), ((), ())), preferred_element_type=F32)
        diag = jnp.zeros((128, 128), F32)
        for k in range(4):
            tile = [
                part[k * 128 : (k + 1) * 128, n * 128 : (n + 1) * 128]
                for n in (k, (k + 1) % 4, (k + 2) % 4)
            ]
            diag = diag + jnp.where(tile_row == tile_col, tile[0], 0.0)
            side = jnp.concatenate(tile[1:], axis=1)
            gram_d[2 * r + k // 2, k % 2] = tile[0].reshape(8, 16, 128).astype(BF16)
            gram_o[2 * r + k // 2, k % 2] = side.reshape(8, 16, 256).astype(BF16)
        lanes = jnp.sum(diag, axis=0, keepdims=True)
        return norms + jnp.where(norm_row == r, jnp.broadcast_to(lanes, (8, 128)), 0.0)

    norms = lax.fori_loop(0, 4, right_gram, jnp.zeros((8, 128), F32))
    norm_own[...] = norms
    lnorm[...] = norms
    get_right.wait()
    for copy in get_rest:
        copy.wait()
    xz[z] = prev_right[...]
    lroot[yl, c] = prev_left[0]

    pl.semaphore_wait(barrier, len(PLANE) + len(DEPTH) + 2)

    for step in DEPTH:
        send(prev_right, xz.at[z], (sent.at[0], got.at[0]), depth_id(step))
    lx_core = send(prev_left.at[0], lroot.at[yl, c], two(sem_l, 0), core_id)
    lx_side = send(prev_left.at[0], lroot.at[yl, c], two(sem_l, 1), side_id)
    for k, step in enumerate(PLANE):
        send(norm_own, norm_p.at[k], (sent.at[3], got.at[1]), plane_id(step))
    n_core = send(lnorm, lnorm_in.at[0], two(sem_l, 2), core_id)
    first = []
    for j, turn in enumerate((2, 1, 3, 0)):
        zz = ((z // 2 + turn) % 4) * 2
        rr = ((me_r + turn) % 4) * 2
        first.append((zz, rr))
        for k in range(7):
            a, b = plane_peer(PLANE[k])
            send(
                gram_o.at[a * 4 + b, :, pl.ds(zz, 2)], plane_in.at[k, j],
                (sent.at[1], got_plane.at[j]), plane_id(PLANE[k]),
            )
            send(
                gram_d.at[pl.ds(rr, 2), :, (z + DEPTH[k]) % 8],
                depth_in.at[k, j], (sent.at[2], got_depth.at[j]), depth_id(DEPTH[k]),
            )

    def left_gram(i, carry):
        rows = grad[pl.ds(pl.multiple_of(i * 128, 128), 128), :]
        part = lax.dot_general(rows, grad[...], (((1,), (1,)), ((), ())), preferred_element_type=F32)
        lgram[i // 2, i % 2] = part.astype(BF16)
        return carry

    lax.fori_loop(0, 4, left_gram, 0)
    l_core = send(lgram.at[:, 1 - c], lin1, two(sem_l, 3), core_id)

    all_here(xz.at[pl.ds(0, 7)], got.at[0])
    x_pass = send(xz.at[:, pl.ds(2 - 2 * yh, 2)], x_across, two(sem_l, 10), plane_id((1, 0)))
    for step in ROW:
        b = (x + step[1]) % 4
        send(xz.at[:, 2 * yh + b // 2], xp.at[p], (sent.at[4], got.at[2]), plane_id(step))
    xp[p] = xz[:, me_r]

    l_core.wait_recv()
    lsum = lgram[:, c].astype(F32) + lin1[...].astype(F32)
    lsend[...] = lsum.astype(BF16)
    l_side = send(lsend.at[1 - yl], lin2, two(sem_l, 6), side_id)
    n_core.wait_recv()
    n_core.wait_send()
    lnorm[...] = lnorm[...] + lnorm_in[0]
    n_side = send(lnorm, lnorm_in.at[1], two(sem_l, 5), side_id)

    all_here(norm_p, got.at[1])
    total = norm_own[...]
    for k in range(7):
        total = total + norm_p[k]
    norm_mid[...] = total
    for k, step in enumerate(DEPTH):
        send(norm_mid, norm_z.at[k], (sent.at[5], got.at[3]), depth_id(step))

    x_pass.wait_recv()
    for step in ROW:
        b = (x + step[1]) % 4
        send(x_across.at[:, b // 2], xp.at[across], (sent.at[4], got.at[2]), plane_id(step))
    xp[across] = x_across[:, x // 2]

    lx_side.wait_recv()
    lx_pass = send(lroot.at[1 - yl, c], lroot.at[1 - yl, c], two(sem_l, 4), core_id)

    for j in range(ROUNDS):
        zz, rr = first[j]
        all_here(plane_in.at[:, j], got_plane.at[j])
        acc = gram_o[p, :, pl.ds(zz, 2)].astype(F32)
        for k in range(7):
            acc = acc + plane_in[k, j].astype(F32)
        plane_sum[:, pl.ds(zz, 2)] = acc.astype(BF16)
        all_here(depth_in.at[:, j], got_depth.at[j])
        acc = gram_d[pl.ds(rr, 2), :, z].astype(F32)
        for k in range(7):
            acc = acc + depth_in[k, j].astype(F32)
        depth_sum[j] = acc.astype(BF16)
        for b in range(2) if j < ROUNDS - 1 else (None,):
            bz = zz + (1 - z % 2 if b is None else b)
            send(plane_sum.at[:, bz], strip_z.at[z], (sent.at[6], got.at[4]), (bz, yh, x, yl, c))
            bp = 1 - p % 2 if b is None else b
            q = rr + bp
            send(depth_sum.at[j, bp], strip_p.at[p], (sent.at[7], got.at[5]),
                 (z, q // 4, q % 4, yl, c))
    strip_z[z] = plane_sum[:, z]
    strip_p[p] = depth_sum[ROUNDS - 1, p % 2]
    for b in range(2):
        block = plane_sum[b, :, :, pl.ds(0, 128)].astype(F32).reshape(128, 128)
        turned[b] = block.T.reshape(8, 16, 128).astype(BF16)
    mate = x + 1 - 2 * (x % 2)
    for step in DEPTH:
        there = (z + step) % 8
        send(turned.at[0, there], miss_b.at[z], (sent.at[12], got.at[9]), depth_id(step))
    for step in (0, *DEPTH):
        there = (z + step) % 8
        send(turned.at[1, there], miss_a.at[z], (sent.at[13], got.at[10]), (there, yh, mate, yl, c))
    miss_b[z] = turned[0, z]

    all_here(xp.at[pl.ds(0, 6)], got.at[2])

    def lay(i, carry):
        rows = xp[:, i].astype(F32).reshape(64, B).astype(BF16)
        root[pl.ds(pl.multiple_of(i * 64, 64), 64), :] = rows
        return carry

    lax.fori_loop(0, 8, lay, 0)

    all_here(norm_z, got.at[3])
    total = norm_mid[...]
    for k in range(7):
        total = total + norm_z[k]
    right_scale = jnp.sum(jnp.where(norm_row == me_r, total, 0.0)) / B + EPSILON

    lx_core.wait_recv()
    lx_pass.wait_recv()
    n_side.wait_recv()
    n_side.wait_send()
    l_side.wait_recv()
    left_scale = jnp.sum(jnp.where(norm_row < 4, lnorm[...] + lnorm_in[1], 0.0)) / B + EPSILON
    left_rows = lsend[yl].astype(F32) + lin2[...].astype(F32)
    product = five_products(left_rows, lroot[...].reshape(B, B)) / left_scale
    left_new = (5.0 * prev_left[0].astype(F32) - product) / 4.0
    left_code = (left_new * pow_two(-exp_left[0])).astype(BF16)
    left_own[...] = left_code

    all_here(strip_z.at[pl.ds(0, 7)], got.at[4])
    all_here(strip_p.at[pl.ds(0, 7)], got.at[5])
    all_here(miss_b.at[pl.ds(0, 7)], got.at[9])
    all_here(miss_a, got.at[10])

    def summed(ref):
        acc = ref[0].astype(F32)
        for k in range(1, 8):
            acc = acc + ref[k].astype(F32)
        return acc

    side, diag, low_a, low_b = summed(strip_z), summed(strip_p), summed(miss_a), summed(miss_b)
    even = p % 2 == 0
    one, two_on = side[:, :, :128], side[:, :, 128:]
    upper = jnp.where(
        even,
        jnp.concatenate([diag[0], one[0], two_on[0], low_a], axis=1),
        jnp.concatenate([two_on[0], low_a, diag[0], one[0]], axis=1),
    )
    lower = jnp.where(
        even,
        jnp.concatenate([low_b, diag[1], one[1], two_on[1]], axis=1),
        jnp.concatenate([one[1], two_on[1], low_b, diag[1]], axis=1),
    )
    rows = jnp.concatenate([upper, lower], axis=0)
    product = five_products(rows, root[...]) / right_scale
    offset = (p % 2) * 256 + z * 16
    start = jnp.concatenate(
        [root[pl.ds(pl.multiple_of(offset + b * 128, 16), 16), :] for b in range(2)], axis=0
    ).astype(F32)
    right_new = (5.0 * start - product) / 4.0
    right_code = (right_new * pow_two(-exp_right[me_r])).reshape(2, 16, B).astype(BF16)
    code[p, :, z] = right_code

    def near(q, layer):
        return code.at[q, :, layer, :, pl.ds(0, CUT)]

    for k, step in enumerate(DEPTH):
        send(near(p, z), near(p, z), (sent.at[8], got_strip.at[k]), depth_id(step))
    for step in PLANE:
        send(code.at[p, :, z], code.at[p, :, z], (sent.at[9], got.at[6]), plane_id(step))
    lcode[yl, c] = left_own[...]
    lc_core = send(left_own, lcode.at[yl, c], two(sem_l, 7), core_id)
    lc_side = send(left_own, lcode.at[yl, c], two(sem_l, 8), side_id)

    def pass_on(i):
        all_here(near(across, (z + 8 - DEPTH[i]) % 8), got_pass.at[i])
        for step in ROW:
            part = near(across, (z + 8 - DEPTH[i]) % 8)
            send(part, part, (sent.at[10], got.at[7]), plane_id(step))

    for i in range(7):
        part = near(p, (z + 8 - DEPTH[i]) % 8)
        all_here(part, got_strip.at[i])
        send(part, part, (sent.at[10], got_pass.at[i]), plane_id((1, 0)))
        for step in ROW:
            send(part, part, (sent.at[10], got.at[7]), plane_id(step))
        if i == 1:
            all_here(code.at[pl.ds(0, 7), :, 0], got.at[6])
            for step in DEPTH:
                part = code.at[:, :, z, :, pl.ds(CUT, B - CUT)]
                send(part, part, (sent.at[11], got.at[8]), depth_id(step))
        if i > 2:
            pass_on(i - 3)
    for i in range(4, 7):
        pass_on(i)
    lc_side.wait_recv()
    lc_pass = send(lcode.at[1 - yl, c], lcode.at[1 - yl, c], two(sem_l, 9), core_id)
    lc_core.wait_recv()
    lc_pass.wait_recv()
    puts = [pltpu.make_async_copy(lcode, left_out, sem_in.at[0])]
    puts[0].start()
    all_here(code.at[pl.ds(0, 6), :, pl.ds(0, 7), :, pl.ds(0, CUT)], got.at[7])
    all_here(code.at[:, :, pl.ds(0, 7), :, pl.ds(CUT, B - CUT)], got.at[8])

    owned = owner_of[z * 8 + p]
    for r in range(4):
        strip = code[2 * r + owned // 32, (owned // 16) % 2, (owned // 2) % 8].astype(F32)
        picked = jnp.where(owned % 2 == 0, strip[:8], strip[8:])
        right_own[r] = picked.astype(BF16)
    puts.append(pltpu.make_async_copy(right_own, right_out, sem_in.at[1]))
    puts[1].start()

    for r in range(4):
        columns = pl.ds(r * B, B)
        full = code[2 * r : 2 * r + 2].reshape(B, B)
        out = jnp.dot(grad[:, columns], full, preferred_element_type=F32)
        middle[:, columns] = (out * pow_two(exp_right[r])).astype(BF16)
        put = pltpu.make_async_copy(middle.at[:, columns], middle_out.at[:, columns], sem_in.at[2 + r])
        put.start()
        puts.append(put)
    for copy in puts:
        copy.wait()

    for k, ref in enumerate((
        xz.at[pl.ds(0, 7)], plane_in, depth_in, norm_p, xp.at[pl.ds(0, 6)], norm_z,
        strip_z.at[pl.ds(0, 7)], strip_p.at[pl.ds(0, 7)],
        code.at[0, :, pl.ds(0, 7), :, pl.ds(0, CUT)], code.at[0, :, pl.ds(0, 7)],
        code.at[pl.ds(0, 7), :, pl.ds(0, 7), :, pl.ds(0, CUT)],
        code.at[:, :, pl.ds(0, 7), :, pl.ds(CUT, B - CUT)],
        miss_b.at[pl.ds(0, 7)], miss_a,
    )):
        all_sent(ref, sent.at[k])
    for copy in (lx_core, lx_side, lx_pass, l_core, l_side, lc_core, lc_side, lc_pass, x_pass):
        copy.wait_send()


def final_kernel(
    exp_left_in, left_in, middle_in, right_in, precond, root_left, root_right,
    exp_left, left, middle, right, out, get_sem, put_sem,
):
    gets = [
        pltpu.make_async_copy(left_in, left, get_sem.at[0]),
        *[
            pltpu.make_async_copy(
                middle_in.at[:, pl.ds(r * B, B)], middle.at[:, pl.ds(r * B, B)], get_sem.at[1 + r]
            )
            for r in range(4)
        ],
        pltpu.make_async_copy(exp_left_in, exp_left, get_sem.at[5]),
        pltpu.make_async_copy(right_in, right, get_sem.at[6]),
    ]
    for get in gets:
        get.start()
    gets[0].wait()
    gets[5].wait()
    gets[6].wait()
    own = left.at[lax.axis_index("yl"), lax.axis_index("c")]
    puts = [
        pltpu.make_async_copy(own, root_left.at[0], put_sem.at[4]),
        pltpu.make_async_copy(right, root_right.at[:, 0], put_sem.at[5]),
    ]
    for put in puts:
        put.start()
    scale = pow_two(exp_left[0])
    for r in range(4):
        columns = pl.ds(r * B, B)
        gets[1 + r].wait()
        part = jnp.dot(left[...].reshape(B, B), middle[:, columns], preferred_element_type=F32)
        out[:, columns] = (part * scale).astype(BF16)
        put = pltpu.make_async_copy(out.at[:, columns], precond.at[:, columns], put_sem.at[r])
        put.start()
        puts.append(put)
    for put in puts:
        put.wait()


def shards(grad, prev_left, prev_right, exp_left, exp_right, strip_owner):
    anywhere = pl.BlockSpec(memory_space=pl.ANY)
    dma = pltpu.SemaphoreType.DMA
    shape = jax.ShapeDtypeStruct
    middle, left_all, right_own = pl.pallas_call(
        exchange_kernel,
        out_shape=(
            shape((B, 4 * B), BF16), shape((2, 2, 128, B), BF16), shape((4, 8, B), BF16),
        ),
        in_specs=[anywhere] * 6,
        out_specs=(anywhere,) * 3,
        scratch_shapes=[
            pltpu.SMEM((1,), jnp.int32), pltpu.SMEM((4,), jnp.int32), pltpu.SMEM((64,), jnp.int32),
            pltpu.VMEM((B, 4 * B), BF16),
            pltpu.VMEM((1, 128, B), BF16),
            pltpu.VMEM((4, 8, B), BF16),
            pltpu.VMEM((B, 4 * B), BF16),
            pltpu.VMEM((128, B), BF16),
            pltpu.VMEM((4, 8, B), BF16),
            pltpu.VMEM((8, 2, 8, 16, 128), BF16),
            pltpu.VMEM((8, 2, 8, 16, 256), BF16),
            pltpu.VMEM((7, ROUNDS, 2, 2, 16, 256), BF16),
            pltpu.VMEM((7, ROUNDS, 2, 2, 16, 128), BF16),
            pltpu.VMEM((2, 8, 16, 256), BF16),
            pltpu.VMEM((ROUNDS, 2, 2, 16, 128), BF16),
            pltpu.VMEM((8, 2, 16, 256), BF16),
            pltpu.VMEM((8, 2, 16, 128), BF16),
            pltpu.VMEM((2, 8, 16, 128), BF16),
            pltpu.VMEM((8, 16, 128), BF16),
            pltpu.VMEM((8, 16, 128), BF16),
            pltpu.VMEM((8, 128), F32),
            pltpu.VMEM((8, 128), F32),
            pltpu.VMEM((7, 8, 128), F32),
            pltpu.VMEM((7, 8, 128), F32),
            pltpu.VMEM((8, 4, 8, B), BF16),
            pltpu.VMEM((8, 2, 8, B), BF16),
            pltpu.VMEM((8, 8, 8, B), BF16),
            pltpu.VMEM((B, B), BF16),
            pltpu.VMEM((8, 2, 8, 16, B), BF16),
            pltpu.VMEM((2, 2, 128, B), BF16),
            pltpu.VMEM((2, 128, B), BF16),
            pltpu.VMEM((2, 128, B), BF16),
            pltpu.VMEM((128, B), BF16),
            pltpu.VMEM((2, 2, 128, B), BF16),
            pltpu.VMEM((2, 2, 128, B), BF16),
            pltpu.VMEM((8, 128), F32),
            pltpu.VMEM((2, 8, 128), F32),
            dma((14,)), dma((11,)), dma((ROUNDS,)), dma((ROUNDS,)), dma((7,)), dma((7,)),
            dma((2, 11)), dma((9,)),
        ],
        compiler_params=pltpu.CompilerParams(
            collective_id=0, has_side_effects=True, vmem_limit_bytes=54 << 20
        ),
        name="exchange",
    )(exp_left, exp_right, strip_owner, grad, prev_left, prev_right)
    return pl.pallas_call(
        final_kernel,
        out_shape=(
            shape((B, 4 * B), BF16), shape((1, 128, B), BF16), shape((4, 1, 8, B), BF16),
        ),
        in_specs=[anywhere] * 4,
        out_specs=(anywhere,) * 3,
        scratch_shapes=[
            pltpu.SMEM((1,), jnp.int32), pltpu.VMEM((2, 2, 128, B), BF16),
            pltpu.VMEM((B, 4 * B), BF16), pltpu.VMEM((4, 8, B), BF16),
            pltpu.VMEM((B, 4 * B), BF16), dma((7,)), dma((6,)),
        ],
        compiler_params=pltpu.CompilerParams(vmem_limit_bytes=54 << 20),
        name="final",
    )(exp_left, left_all, middle, right_own)


def solution(mesh):
    torus = Mesh(mesh.devices.reshape(8, 2, 4, 2, 2), AXES)
    in_specs = (
        P(GROUP, REPLICA),
        P(GROUP, REPLICA, None),
        P(REPLICA, GROUP, None),
        P(GROUP),
        P(REPLICA),
        P(),
    )
    out_specs = (P(GROUP, REPLICA), P(GROUP, REPLICA, None), P(REPLICA, GROUP, None, None))
    return jax.shard_map(
        shards, mesh=torus, in_specs=in_specs, out_specs=out_specs, check_vma=False
    )
```

time: 89 us -> 65.5 us (0.74)
  Pallas kernels: 79.4 us -> 64 us
  local copies, waits for them, and re-layouts: 7.95 us -> 0 us
    pallas_call x1, Pallas kernels: 74.6 us -> 59.8 us  [shards(): pl.pallas_call(exchange_kernel, out_shape=(shape((B, 4 * B), BF16), shape...]
    unnamed x18 -> x0, local copies, waits for them, and re-layouts: 7.95 us -> none
where the time goes in v2:
time: 65.5 us; the launch traced here: 65.3 us
  Pallas kernels  64 us (98%)
  between operations  1.29 us (2%)
    pallas_call x1, Pallas kernels, shards(): pl.pallas_call(exchange_kernel, out_shape=(shape((B, 4 * B), BF16), shape...  59.8 us
    pallas_call x1, Pallas kernels, shards(): pl.pallas_call(final_kernel, out_shape=(shape((B, 4 * B), BF16), shape((1...  4.25 us

profile of v2, /device:TPU:32, one launch (start us, length us, event | category | flops | bytes accessed | tf_op | source)
XLA Modules:
  0.0 65.3 jit_solution(12278516707594650096)
XLA Ops:
  1.3 59.8 %exchange.1 = (bf16[512,2048]{1,0:T(8,128)(2,1)}, bf16[2,2,128,512]{3,2,1,0:T(8,128)(2,1)}, bf16[4,8,512]{2,1,0:T(8,128)(2,1)}) custom-call(s32[1]{0:T(128)S(6)} %copy.9.exp_left_in, s32[4]{0:T(128)} %exp_right_in.1, s32[64]{0:T(128)} %owner_in.1, bf16[512,2048]{1,0:T(8,128)(2,1)} %grad_in.1, bf16[1,128,512]{2,1,0:T(8,128)(2,1)} %prev_left_in.1, ...), custom_call_target="tpu_custom_call" | custom-call | tf_op jit(solution)/shard_map/exchange/pallas_call | solution.py:431
  61.1 4.2 %final.1 = (bf16[512,2048]{1,0:T(8,128)(2,1)}, bf16[1,128,512]{2,1,0:T(8,128)(2,1)}, bf16[4,1,8,512]{3,2,1,0:T(8,128)(2,1)}) custom-call(s32[1]{0:T(128)S(6)} %copy.9.exp_left_in, bf16[2,2,128,512]{3,2,1,0:T(8,128)(2,1)} %get-tuple-element.6.left_in, bf16[512,2048]{1,0:T(8,128)(2,1)} %get-tuple-element.7.middle_in, bf16[4,8,512]{2,1,0:T(8,128)(2,1)} %get-tuple-element.8.right_in), custom_call_target="tpu_custom_call" | custom-call | tf_op jit(solution)/shard_map/final/pallas_call | solution.py:482

commit v3 on v2

--- a/solution.py
+++ b/solution.py
@@ -21,6 +21,7 @@
 ROUNDS = 4
 PLANE = ((0, 1), (1, 0), (0, 3), (0, 2), (1, 1), (1, 3), (1, 2))
 ROW = ((0, 1), (0, 3), (0, 2))
+X_FIRST = (7, 0, 1)
 DEPTH = (1, 7, 2, 6, 3, 5, 4)
 
 
@@ -51,7 +52,7 @@
     norm_own, norm_mid, norm_p, norm_z,
     xz, x_across, xp, root, code,
     lgram, lin1, lsend, lin2, lroot, lcode, lnorm, lnorm_in,
-    sent, got, got_plane, got_depth, got_strip, got_pass, sem_l, sem_in,
+    sent, got, got_plane, got_depth, got_strip, got_pass, got_row, sem_l, sem_in,
 ):
     z, yh, x = lax.axis_index("z"), lax.axis_index("yh"), lax.axis_index("x")
     yl, c = lax.axis_index("yl"), lax.axis_index("c")
@@ -155,25 +156,30 @@
     for step in DEPTH:
         send(prev_right, xz.at[z], (sent.at[0], got.at[0]), depth_id(step))
     lx_core = send(prev_left.at[0], lroot.at[yl, c], two(sem_l, 0), core_id)
-    lx_side = send(prev_left.at[0], lroot.at[yl, c], two(sem_l, 1), side_id)
     for k, step in enumerate(PLANE):
         send(norm_own, norm_p.at[k], (sent.at[3], got.at[1]), plane_id(step))
     n_core = send(lnorm, lnorm_in.at[0], two(sem_l, 2), core_id)
-    first = []
-    for j, turn in enumerate((2, 1, 3, 0)):
-        zz = ((z // 2 + turn) % 4) * 2
-        rr = ((me_r + turn) % 4) * 2
-        first.append((zz, rr))
+    first = [
+        (((z // 2 + turn) % 4) * 2, ((me_r + turn) % 4) * 2) for turn in (2, 1, 3, 0)
+    ]
+
+    def plane_round(j):
         for k in range(7):
             a, b = plane_peer(PLANE[k])
             send(
-                gram_o.at[a * 4 + b, :, pl.ds(zz, 2)], plane_in.at[k, j],
+                gram_o.at[a * 4 + b, :, pl.ds(first[j][0], 2)], plane_in.at[k, j],
                 (sent.at[1], got_plane.at[j]), plane_id(PLANE[k]),
             )
+
+    def depth_round(j):
+        for k in range(7):
             send(
-                gram_d.at[pl.ds(rr, 2), :, (z + DEPTH[k]) % 8],
+                gram_d.at[pl.ds(first[j][1], 2), :, (z + DEPTH[k]) % 8],
                 depth_in.at[k, j], (sent.at[2], got_depth.at[j]), depth_id(DEPTH[k]),
             )
+
+    for j in range(3):
+        plane_round(j)
 
     def left_gram(i, carry):
         rows = grad[pl.ds(pl.multiple_of(i * 128, 128), 128), :]
@@ -183,14 +189,19 @@
 
     lax.fori_loop(0, 4, left_gram, 0)
     l_core = send(lgram.at[:, 1 - c], lin1, two(sem_l, 3), core_id)
+    depth_round(0)
 
     all_here(xz.at[pl.ds(0, 7)], got.at[0])
     x_pass = send(xz.at[:, pl.ds(2 - 2 * yh, 2)], x_across, two(sem_l, 10), plane_id((1, 0)))
+    plane_round(3)
     for step in ROW:
         b = (x + step[1]) % 4
         send(xz.at[:, 2 * yh + b // 2], xp.at[p], (sent.at[4], got.at[2]), plane_id(step))
+    for j in range(1, ROUNDS):
+        depth_round(j)
     xp[p] = xz[:, me_r]
 
+    lx_side = send(prev_left.at[0], lroot.at[yl, c], two(sem_l, 1), side_id)
     l_core.wait_recv()
     lsum = lgram[:, c].astype(F32) + lin1[...].astype(F32)
     lsend[...] = lsum.astype(BF16)
@@ -213,9 +224,6 @@
         b = (x + step[1]) % 4
         send(x_across.at[:, b // 2], xp.at[across], (sent.at[4], got.at[2]), plane_id(step))
     xp[across] = x_across[:, x // 2]
-
-    lx_side.wait_recv()
-    lx_pass = send(lroot.at[1 - yl, c], lroot.at[1 - yl, c], two(sem_l, 4), core_id)
 
     for j in range(ROUNDS):
         zz, rr = first[j]
@@ -250,6 +258,9 @@
         send(turned.at[1, there], miss_a.at[z], (sent.at[13], got.at[10]), (there, yh, mate, yl, c))
     miss_b[z] = turned[0, z]
 
+    lx_side.wait_recv()
+    lx_pass = send(lroot.at[1 - yl, c], lroot.at[1 - yl, c], two(sem_l, 4), core_id)
+
     all_here(xp.at[pl.ds(0, 6)], got.at[2])
 
     def lay(i, carry):
@@ -264,18 +275,6 @@
     for k in range(7):
         total = total + norm_z[k]
     right_scale = jnp.sum(jnp.where(norm_row == me_r, total, 0.0)) / B + EPSILON
-
-    lx_core.wait_recv()
-    lx_pass.wait_recv()
-    n_side.wait_recv()
-    n_side.wait_send()
-    l_side.wait_recv()
-    left_scale = jnp.sum(jnp.where(norm_row < 4, lnorm[...] + lnorm_in[1], 0.0)) / B + EPSILON
-    left_rows = lsend[yl].astype(F32) + lin2[...].astype(F32)
-    product = five_products(left_rows, lroot[...].reshape(B, B)) / left_scale
-    left_new = (5.0 * prev_left[0].astype(F32) - product) / 4.0
-    left_code = (left_new * pow_two(-exp_left[0])).astype(BF16)
-    left_own[...] = left_code
 
     all_here(strip_z.at[pl.ds(0, 7)], got.at[4])
     all_here(strip_p.at[pl.ds(0, 7)], got.at[5])
@@ -316,41 +315,96 @@
 
     for k, step in enumerate(DEPTH):
         send(near(p, z), near(p, z), (sent.at[8], got_strip.at[k]), depth_id(step))
+    far = code.at[p, :, z, :, pl.ds(CUT, B - CUT)]
     for step in PLANE:
-        send(code.at[p, :, z], code.at[p, :, z], (sent.at[9], got.at[6]), plane_id(step))
+        send(far, far, (sent.at[9], got.at[6]), plane_id(step))
+    layers = [(z + 8 - step) % 8 for step in DEPTH] + [z]
+
+    def spread(i):
+        part = near(p, layers[i])
+        if i in X_FIRST:
+            for step in ROW:
+                send(part, part, (sent.at[10], got_row.at[X_FIRST.index(i)]), plane_id(step))
+            return
+        send(part, part, (sent.at[10], got_pass.at[i]), plane_id((1, 0)))
+        for step in ROW:
+            send(part, part, (sent.at[10], got.at[7]), plane_id(step))
+
+    def cross(i):
+        all_here(code.at[pl.ds(0, 3), :, 0, :, pl.ds(0, CUT)], got_row.at[X_FIRST.index(i)])
+        for n in range(4):
+            part = near(yh * 4 + n, layers[i])
+            send(part, part, (sent.at[10], got.at[12]), plane_id((1, 0)))
+
+    def pass_on(i):
+        part = near(across, layers[i])
+        all_here(part, got_pass.at[i])
+        for step in ROW:
+            send(part, part, (sent.at[10], got.at[11]), plane_id(step))
+
+    spread(7)
+
+    lx_core.wait_recv()
+    lx_pass.wait_recv()
+    n_side.wait_recv()
+    n_side.wait_send()
+    l_side.wait_recv()
+    left_scale = jnp.sum(jnp.where(norm_row < 4, lnorm[...] + lnorm_in[1], 0.0)) / B + EPSILON
+    left_rows = lsend[yl].astype(F32) + lin2[...].astype(F32)
+    product = five_products(left_rows, lroot[...].reshape(B, B)) / left_scale
+    left_new = (5.0 * prev_left[0].astype(F32) - product) / 4.0
+    left_code = (left_new * pow_two(-exp_left[0])).astype(BF16)
+    left_own[...] = left_code
+
     lcode[yl, c] = left_own[...]
     lc_core = send(left_own, lcode.at[yl, c], two(sem_l, 7), core_id)
     lc_side = send(left_own, lcode.at[yl, c], two(sem_l, 8), side_id)
 
-    def pass_on(i):
-        all_here(near(across, (z + 8 - DEPTH[i]) % 8), got_pass.at[i])
-        for step in ROW:
-            part = near(across, (z + 8 - DEPTH[i]) % 8)
-            send(part, part, (sent.at[10], got.at[7]), plane_id(step))
-
     for i in range(7):
-        part = near(p, (z + 8 - DEPTH[i]) % 8)
-        all_here(part, got_strip.at[i])
-        send(part, part, (sent.at[10], got_pass.at[i]), plane_id((1, 0)))
-        for step in ROW:
-            send(part, part, (sent.at[10], got.at[7]), plane_id(step))
+        all_here(near(p, layers[i]), got_strip.at[i])
+        spread(i)
         if i == 1:
-            all_here(code.at[pl.ds(0, 7), :, 0], got.at[6])
+            all_here(code.at[pl.ds(0, 7), :, 0, :, pl.ds(CUT, B - CUT)], got.at[6])
             for step in DEPTH:
                 part = code.at[:, :, z, :, pl.ds(CUT, B - CUT)]
                 send(part, part, (sent.at[11], got.at[8]), depth_id(step))
-        if i > 2:
+            cross(7)
+        if i in (3, 4):
+            cross(i - 3)
+        if i == 4:
+            lc_side.wait_recv()
+            lc_pass = send(lcode.at[1 - yl, c], lcode.at[1 - yl, c], two(sem_l, 9), core_id)
+        if i > 4:
             pass_on(i - 3)
     for i in range(4, 7):
         pass_on(i)
-    lc_side.wait_recv()
-    lc_pass = send(lcode.at[1 - yl, c], lcode.at[1 - yl, c], two(sem_l, 9), core_id)
     lc_core.wait_recv()
     lc_pass.wait_recv()
     puts = [pltpu.make_async_copy(lcode, left_out, sem_in.at[0])]
     puts[0].start()
-    all_here(code.at[pl.ds(0, 6), :, pl.ds(0, 7), :, pl.ds(0, CUT)], got.at[7])
+    def mix(r, index, whole):
+        columns = pl.ds(pl.multiple_of(r * B, B), B)
+        full = code[pl.ds(2 * r, 2)].reshape(B, B)
+        out = jnp.dot(grad[:, columns], full, preferred_element_type=F32)
+        out = (out * pow_two(exp_right[r])).astype(BF16)
+        if whole:
+            out = jnp.dot(lcode[...].reshape(B, B), out, preferred_element_type=F32)
+            out = (out * pow_two(exp_left[0])).astype(BF16)
+        middle[:, columns] = out
+        put = pltpu.make_async_copy(
+            middle.at[:, columns], middle_out.at[:, columns], sem_in.at[2 + index]
+        )
+        put.start()
+        puts.append(put)
+
     all_here(code.at[:, :, pl.ds(0, 7), :, pl.ds(CUT, B - CUT)], got.at[8])
+    all_here(code.at[pl.ds(0, 3), :, pl.ds(0, 5), :, pl.ds(0, CUT)], got.at[7])
+    for b in range(2):
+        mix(2 * yh + b, b, True)
+    all_here(code.at[pl.ds(0, 4), :, pl.ds(0, 3), :, pl.ds(0, CUT)], got.at[12])
+    all_here(code.at[pl.ds(0, 3), :, pl.ds(0, 5), :, pl.ds(0, CUT)], got.at[11])
+    for b in range(2):
+        mix(2 - 2 * yh + b, 2 + b, False)
 
     owned = owner_of[z * 8 + p]
     for r in range(4):
@@ -358,24 +412,15 @@
         picked = jnp.where(owned % 2 == 0, strip[:8], strip[8:])
         right_own[r] = picked.astype(BF16)
     puts.append(pltpu.make_async_copy(right_own, right_out, sem_in.at[1]))
-    puts[1].start()
-
-    for r in range(4):
-        columns = pl.ds(r * B, B)
-        full = code[2 * r : 2 * r + 2].reshape(B, B)
-        out = jnp.dot(grad[:, columns], full, preferred_element_type=F32)
-        middle[:, columns] = (out * pow_two(exp_right[r])).astype(BF16)
-        put = pltpu.make_async_copy(middle.at[:, columns], middle_out.at[:, columns], sem_in.at[2 + r])
-        put.start()
-        puts.append(put)
+    puts[-1].start()
     for copy in puts:
         copy.wait()
 
     for k, ref in enumerate((
         xz.at[pl.ds(0, 7)], plane_in, depth_in, norm_p, xp.at[pl.ds(0, 6)], norm_z,
         strip_z.at[pl.ds(0, 7)], strip_p.at[pl.ds(0, 7)],
-        code.at[0, :, pl.ds(0, 7), :, pl.ds(0, CUT)], code.at[0, :, pl.ds(0, 7)],
-        code.at[pl.ds(0, 7), :, pl.ds(0, 7), :, pl.ds(0, CUT)],
+        code.at[0, :, pl.ds(0, 7), :, pl.ds(0, CUT)], code.at[0, :, pl.ds(0, 7), :, pl.ds(CUT, B - CUT)],
+        code.at[pl.ds(0, 7), :, :, :, pl.ds(0, CUT)],
         code.at[:, :, pl.ds(0, 7), :, pl.ds(CUT, B - CUT)],
         miss_b.at[pl.ds(0, 7)], miss_a,
     )):
@@ -388,12 +433,15 @@
     exp_left_in, left_in, middle_in, right_in, precond, root_left, root_right,
     exp_left, left, middle, right, out, get_sem, put_sem,
 ):
+    yh = lax.axis_index("yh")
+    blocks = [
+        pl.ds(pl.multiple_of((2 - 2 * yh + r % 2 if r < 2 else 2 * yh + r % 2) * B, B), B)
+        for r in range(4)
+    ]
     gets = [
         pltpu.make_async_copy(left_in, left, get_sem.at[0]),
         *[
-            pltpu.make_async_copy(
-                middle_in.at[:, pl.ds(r * B, B)], middle.at[:, pl.ds(r * B, B)], get_sem.at[1 + r]
-            )
+            pltpu.make_async_copy(middle_in.at[:, blocks[r]], middle.at[:, blocks[r]], get_sem.at[1 + r])
             for r in range(4)
         ],
         pltpu.make_async_copy(exp_left_in, exp_left, get_sem.at[5]),
@@ -413,11 +461,12 @@
         put.start()
     scale = pow_two(exp_left[0])
     for r in range(4):
-        columns = pl.ds(r * B, B)
         gets[1 + r].wait()
-        part = jnp.dot(left[...].reshape(B, B), middle[:, columns], preferred_element_type=F32)
-        out[:, columns] = (part * scale).astype(BF16)
-        put = pltpu.make_async_copy(out.at[:, columns], precond.at[:, columns], put_sem.at[r])
+        if r < 2:
+            part = jnp.dot(left[...].reshape(B, B), middle[:, blocks[r]], preferred_element_type=F32)
+            out[:, blocks[r]] = (part * scale).astype(BF16)
+        source = out if r < 2 else middle
+        put = pltpu.make_async_copy(source.at[:, blocks[r]], precond.at[:, blocks[r]], put_sem.at[r])
         put.start()
         puts.append(put)
     for put in puts:
@@ -471,7 +520,7 @@
             pltpu.VMEM((2, 2, 128, B), BF16),
             pltpu.VMEM((8, 128), F32),
             pltpu.VMEM((2, 8, 128), F32),
-            dma((14,)), dma((11,)), dma((ROUNDS,)), dma((ROUNDS,)), dma((7,)), dma((7,)),
+            dma((14,)), dma((13,)), dma((ROUNDS,)), dma((ROUNDS,)), dma((7,)), dma((7,)), dma((3,)),
             dma((2, 11)), dma((9,)),
         ],
         compiler_params=pltpu.CompilerParams(

time: 65.5 us -> 64.1 us (0.979)
  Pallas kernels: 64 us -> 62.6 us
    pallas_call x1, Pallas kernels: 59.8 us -> 58.9 us  [shards(): pl.pallas_call(exchange_kernel, out_shape=(shape((B, 4 * B), BF16), shape...]
where the time goes in v3:
time: 64.1 us; the launch traced here: 63.9 us
  Pallas kernels  62.6 us (98%)
  between operations  1.29 us (2%)
    pallas_call x1, Pallas kernels, shards(): pl.pallas_call(exchange_kernel, out_shape=(shape((B, 4 * B), BF16), shape...  58.9 us
    pallas_call x1, Pallas kernels, shards(): pl.pallas_call(final_kernel, out_shape=(shape((B, 4 * B), BF16), shape((1...  3.7 us

profile of v3, /device:TPU:32, one launch (start us, length us, event | category | flops | bytes accessed | tf_op | source)
XLA Modules:
  0.0 63.9 jit_solution(15177697128613167617)
XLA Ops:
  1.3 58.9 %exchange.1 = (bf16[512,2048]{1,0:T(8,128)(2,1)}, bf16[2,2,128,512]{3,2,1,0:T(8,128)(2,1)}, bf16[4,8,512]{2,1,0:T(8,128)(2,1)}) custom-call(s32[1]{0:T(128)S(6)} %copy.9.exp_left_in, s32[4]{0:T(128)} %exp_right_in.1, s32[64]{0:T(128)} %owner_in.1, bf16[512,2048]{1,0:T(8,128)(2,1)} %grad_in.1, bf16[1,128,512]{2,1,0:T(8,128)(2,1)} %prev_left_in.1, ...), custom_call_target="tpu_custom_call" | custom-call | tf_op jit(solution)/shard_map/exchange/pallas_call | solution.py:480
  60.2 3.7 %final.1 = (bf16[512,2048]{1,0:T(8,128)(2,1)}, bf16[1,128,512]{2,1,0:T(8,128)(2,1)}, bf16[4,1,8,512]{3,2,1,0:T(8,128)(2,1)}) custom-call(s32[1]{0:T(128)S(6)} %copy.9.exp_left_in, bf16[2,2,128,512]{3,2,1,0:T(8,128)(2,1)} %get-tuple-element.6.left_in, bf16[512,2048]{1,0:T(8,128)(2,1)} %get-tuple-element.7.middle_in, bf16[4,8,512]{2,1,0:T(8,128)(2,1)} %get-tuple-element.8.right_in), custom_call_target="tpu_custom_call" | custom-call | tf_op jit(solution)/shard_map/final/pallas_call | solution.py:531
